TPU v7x, 32 devices: a whole 2x2x4 slice. The times are simulated.
32 devices in a mesh: prow: 4 (over y, x), pcol: 8 (over z, core).
Axes of the slice: x: 2, y: 2, z: 4, core: 2. Of those that a mesh axis runs over, the one named last changes fastest.
Arguments:
- covariance: float32 [16384, 16384], P(('prow', 'pcol')), may hold values from -600 to 600, as said below
- factor_left: float32 [64, 16384], P(None, ('prow', 'pcol')), may hold values from -6 to 6
- factor_right: float32 [64, 16384], P('prow', 'pcol'), may hold values from -3 to 3
Outputs:
- whitened: float32 [16384, 16384], P('prow', 'pcol')
Inputs may be any that keep to these rules, and one draw needn't show every extreme that they name: `covariance`: entries are real-valued and of full rank.
All inputs are finite; a program needn't handle non-finite values.
Results may differ from a plain program's by a relative error of at most 0.00007.
Values sent between devices are 32-bit elements; how exact they have to be, the bound alone decides.
A program may use at most 192 MiB of HBM per device.

v0:
```python
import jax
import jax.numpy as jnp
from jax import lax
from jax.sharding import PartitionSpec as P

ORDER = 16384
TILE = 64
epsilon = 1e-06


def deal_columns(source):
    height = source.shape[0]
    breadth = source.shape[1]
    grid_cols = lax.axis_size("pcol")
    arranged = (
        source.reshape(height, breadth // (TILE * grid_cols), grid_cols, TILE)
        .transpose(0, 2, 1, 3)
        .reshape(height, breadth)
    )
    return lax.all_to_all(arranged, "pcol", split_axis=1, concat_axis=0, tiled=True)


def order_rows(source):
    height = source.shape[0]
    breadth = source.shape[1]
    grid_rows = lax.axis_size("prow")
    grouped = source.reshape(height // (TILE * grid_rows), grid_rows, TILE, breadth)
    return grouped.transpose(1, 0, 2, 3).reshape(height, breadth)


def body(covariance, factor_left, factor_right):
    right_panel = lax.all_gather(factor_right, "prow", axis=0, tiled=True)
    dealt = deal_columns(covariance)
    left_block = lax.all_gather(factor_left, "pcol", axis=1, tiled=True).T
    tiles_moved, left_rows = (
        lax.all_to_all(order_rows(dealt), "prow", split_axis=0, concat_axis=0, tiled=True),
        lax.all_to_all(order_rows(left_block), "prow", split_axis=0, concat_axis=0, tiled=True),
    )
    corrected = tiles_moved + jnp.dot(
        left_rows, right_panel, precision=lax.Precision.HIGHEST, preferred_element_type=jnp.float32
    )
    squared = corrected * corrected
    row_total = lax.psum(jnp.sum(squared, axis=1), "pcol")
    col_total = lax.psum(jnp.sum(squared, axis=0), "prow")
    row_mean = row_total / ORDER + epsilon
    col_mean = col_total / ORDER + epsilon
    return corrected * lax.rsqrt(jnp.sqrt(row_mean[:, None] * col_mean[None, :]))


def solution(mesh):
    placed = (P(("prow", "pcol"), None), P(None, ("prow", "pcol")), P("prow", "pcol"))
    return jax.shard_map(
        body, mesh=mesh, in_specs=placed, out_specs=P("prow", "pcol"), check_vma=False
    )
```

profile of v0, /device:TPU:0, one launch (start us, length us, event | category | flops | bytes accessed | tf_op | source)
XLA Modules:
  0.0 1344.6 jit_solution(4344010486472771985)
XLA Ops:
  6.5 33.4 %copy.8 = f32[512,16384]{0,1:T(8,128)} copy(f32[512,16384]{1,0:T(8,128)} %param.3) | data formatting | bytes 67108864 | tf_op args[0]
  40.0 23.8 %copy.9 = f32[512,8,32,64]{0,3,2,1:T(8,128)} copy(f32[512,8,32,64]{0,3,1,2:T(8,128)} %bitcast.28) | data formatting | bytes 67108864 | tf_op jit(solution)/shard_map/transpose | solution.py:17
  63.7 7.1 all-to-all-start
  70.8 0.0 all-gather.2.cloned.1.call-start
  70.8 0.7 all-gather.2.cloned.1.call-update
  71.5 36.2 %all-gather.2.cloned.1.call-done = f32[64,4096]{1,0:T(8,128)} async-done(((f32[64,512]{1,0:T(8,128)}), f32[64,4096]{1,0:T(8,128)}) %all-gather.2.cloned.1.call-update) | async-done | bytes 1048592 | tf_op jit(solution)/shard_map/all_gather | solution.py:34
  107.8 2.6 reshape.27
  110.4 1.5 copy.16
  111.9 2.8 all_to_all.34
  114.6 688.7 %all-to-all-done = f32[512,8,2048]{0,2,1:T(8,128)} async-done(((f32[512,8,2048]{0,2,1:T(8,128)}), f32[512,8,2048]{0,2,1:T(8,128)}, u32[]{:S(2)}, u32[]{:S(2)}) %all-to-all-start) | async-done | bytes 33554464 | tf_op jit(solution)/shard_map/all_to_all | solution.py:20
  803.3 4.3 all-to-all-start.2
  807.6 31.7 %copy.10 = f32[8,512,2048]{2,1,0:T(8,128)} copy(f32[8,512,2048]{1,2,0:T(8,128)} %bitcast.3) | data formatting | bytes 67108864 | tf_op jit(solution)/shard_map/all_to_all | solution.py:20
  839.3 23.0 %copy.11 = f32[4,16,64,2048]{3,2,1,0:T(8,128)} copy(f32[4,16,64,2048]{3,2,0,1:T(8,128)} %bitcast.27) | data formatting | bytes 67108864 | tf_op jit(solution)/shard_map/transpose | solution.py:28
  862.3 0.0 all-to-all-done.2
  862.3 0.0 copy-start
  862.3 9.8 all-to-all-start.1
  872.1 0.0 copy-done
  872.2 367.5 %all_gather.7 = f32[64,2048]{1,0:T(8,128)S(1)} all-gather(f32[16,2048]{1,0:T(8,128)S(1)} %copy-done), channel_id=1, replica_groups=mesh['prow'=4,'pcol'=8] {'prow'}, dimensions={0}, use_global_device_ids=true | all-gather | bytes 655360 | tf_op jit(solution)/shard_map/all_gather | solution.py:32
  1239.6 0.1 copy.14
  1239.8 0.0 all-to-all-done.1
  1239.8 35.9 %multiply_reduce_fusion.1 = (f32[4096]{0:T(1024)S(1)}, f32[2048]{0:T(1024)S(1)}, f32[4096,2048]{1,0:T(8,128)}) fusion(f32[4096,64]{0,1:T(8,128)S(1)} %bitcast.30, f32[64,2048]{1,0:T(8,128)S(1)} %all_gather.7, f32[4,1024,2048]{2,1,0:T(8,128)} %all-to-all-done.1), kind=kOutput, calls=%fused_computation.3 | convolution fusion | flops 6475999232 | bytes 68706304 | tf_op jit(solution)/shard_map/dot_general | solution.py:39
  1275.6 25.9 %psum.14 = f32[4096]{0:T(1024)S(1)} all-reduce(f32[4096]{0:T(1024)S(1)} %get-tuple-element.5), channel_id=1, replica_groups=mesh['prow'=4,'pcol'=8] {'pcol'}, use_global_device_ids=true, to_apply=%region_1.0 | all-reduce | flops 4096 | bytes 32768 | tf_op jit(solution)/shard_map/psum | solution.py:43
  1301.5 9.1 psum.15
  1310.6 27.1 %rsqrt_multiply_fusion = f32[4096,2048]{1,0:T(8,128)} fusion(f32[4096,2048]{1,0:T(8,128)} %get-tuple-element.7, f32[2048]{0:T(1024)S(1)} %multiply_add_fusion.1, f32[4096]{0:T(1024)S(1)} %multiply_add_fusion), kind=kLoop, calls=%fused_computation.1 | loop fusion | flops 16777216 | bytes 67133440 | tf_op jit(solution)/shard_map/mul | solution.py:47
  (2 shorter events, 0.0 us)
Async XLA Ops:
  63.7 739.5 %all-to-all-start = ((f32[512,8,2048]{0,2,1:T(8,128)}), f32[512,8,2048]{0,2,1:T(8,128)}, u32[]{:S(2)}, u32[]{:S(2)}) async-start(f32[512,8,2048]{0,2,1:T(8,128)} %bitcast.25), calls=%async_computation | async-start | bytes 67108864 | tf_op jit(solution)/shard_map/all_to_all | solution.py:20
  70.8 36.9 %all-gather.2.cloned.1.call-start = ((), (), s32[]{:S(2)}) async-start(), calls=%async_computation.3 | async-start | bytes 1179648 | tf_op jit(solution)/shard_map/all_gather | solution.py:34
  803.3 59.0 %all-to-all-start.2 = ((f32[4,1024,64]{1,2,0:T(8,128)}), f32[4,1024,64]{1,2,0:T(8,128)S(1)}, u32[]{:S(2)}, u32[]{:S(2)}) async-start(f32[4,1024,64]{1,2,0:T(8,128)} %all_to_all.34), calls=%async_computation.2 | async-start | bytes 2097152 | tf_op jit(solution)/shard_map/all_to_all | solution.py:37
  862.3 9.8 copy-start
  862.3 377.4 %all-to-all-start.1 = ((f32[4,1024,2048]{2,1,0:T(8,128)}), f32[4,1024,2048]{2,1,0:T(8,128)}, u32[]{:S(2)}, u32[]{:S(2)}) async-start(f32[4,1024,2048]{2,1,0:T(8,128)} %bitcast.26), calls=%async_computation.1 | async-start | bytes 67108864 | tf_op jit(solution)/shard_map/all_to_all | solution.py:36
Sparse Core Ops, SparseCore 0:
  73.2 34.4 all-gather.1
where the time goes:
time: 1350 us; the launch traced here: 1340 us
  waiting for transfers between devices  726 us (54%)
  blocking collectives  402 us (30%)
  local copies, waits for them, and re-layouts  119 us (9%)
  matrix products  35.9 us (3%)
  other arithmetic  27.1 us (2%)
  starting transfers between devices  21.2 us (2%)
  between operations  13.5 us (1%)
    all_to_all x1, waiting for transfers between devices, deal_columns(): lax.all_to_all(arranged, 'pcol', split_axis=1, concat_axis=0, tiled=True)  689 us
    all_gather x1, blocking collectives, body(): right_panel = lax.all_gather(factor_right, 'prow', axis=0, tiled=True)  367 us
    all_gather x1, waiting for transfers between devices, body(): left_block = lax.all_gather(factor_left, 'pcol', axis=1, tiled=True).T  36.2 us
    dot_general x1, matrix products, body(): jnp.dot(left_rows, right_panel, precision=lax.Precision.HIGHEST, preferre...  35.9 us
    unnamed x3, local copies, waits for them, and re-layouts  33.4 us
    all_to_all x1, local copies, waits for them, and re-layouts, deal_columns(): lax.all_to_all(arranged, 'pcol', split_axis=1, concat_axis=0, tiled=True)  31.7 us
    mul x1, other arithmetic, body(): corrected * lax.rsqrt(jnp.sqrt(row_mean[:, None] * col_mean[None, :]))  27.1 us
  transfers between devices with their start and end apart: 4, of which 2 were waited for; matrix products, arithmetic and copies ran while one was open for 4% of the time, Pallas kernels for 0%

commit v1 on v0

--- a/solution.py
+++ b/solution.py
@@ -6,6 +6,16 @@
 ORDER = 16384
 TILE = 64
 epsilon = 1e-06
+
+
+def around_the_ring(x, mesh_axis, along):
+    size = lax.axis_size(mesh_axis)
+    block, parts = (x, [x])
+    for _ in range(size - 1):
+        block = lax.ppermute(block, mesh_axis, [(i, (i + 1) % size) for i in range(size)])
+        parts.insert(0, block)
+    row_of_blocks = jnp.concatenate(parts, axis=along)
+    return jnp.roll(row_of_blocks, (lax.axis_index(mesh_axis) + 1) * x.shape[along], axis=along)
 
 
 def deal_columns(source):
@@ -29,7 +39,7 @@
 
 
 def body(covariance, factor_left, factor_right):
-    right_panel = lax.all_gather(factor_right, "prow", axis=0, tiled=True)
+    right_panel = around_the_ring(factor_right, "prow", 0)
     dealt = deal_columns(covariance)
     left_block = lax.all_gather(factor_left, "pcol", axis=1, tiled=True).T
     tiles_moved, left_rows = (

time: 1350 us -> 1420 us (1.052)
  waiting for transfers between devices: 726 us -> 1100 us
  blocking collectives: 402 us -> 33.5 us
  local copies, waits for them, and re-layouts: 119 us -> 183 us
    ppermute x0 -> x3, waiting for transfers between devices: none -> 375 us  [around_the_ring(): lax.ppermute(block, mesh_axis, [(i, (i + 1) % size) for i in range(size)])]
    all_gather x1 -> x0, blocking collectives: 367 us -> none  [body(): right_panel = lax.all_gather(factor_right, 'prow', axis=0, tiled=True)]
    mul x0 -> x1, local copies, waits for them, and re-layouts: none -> 33.3 us  [body(): corrected * lax.rsqrt(jnp.sqrt(row_mean[:, None] * col_mean[None, :]))]
    all_to_all x0 -> x1, local copies, waits for them, and re-layouts: none -> 31.1 us  [body(): lax.all_to_all(order_rows(dealt), 'prow', split_axis=0, concat_axis=0, ti...]
    unnamed x3 -> x10, local copies, waits for them, and re-layouts: 33.4 us -> 33.5 us
  transfers between devices with their start and end apart: 4 -> 7, of which waited for: 2 -> 5; matrix products, arithmetic and copies ran while one was open for 4% -> 4% of each run, Pallas kernels for 0% -> 0%
where the time goes in v1:
time: 1420 us
  waiting for transfers between devices  1100 us (77%)
  local copies, waits for them, and re-layouts  183 us (13%)
  matrix products  36 us (3%)
  blocking collectives  33.5 us (2%)
  other arithmetic  26.6 us (2%)
  starting transfers between devices  23.3 us (2%)
    all_to_all x1, waiting for transfers between devices, deal_columns(): lax.all_to_all(arranged, 'pcol', split_axis=1, concat_axis=0, tiled=True)  689 us
    ppermute x3, waiting for transfers between devices, around_the_ring(): lax.ppermute(block, mesh_axis, [(i, (i + 1) % size) for i in range(size)])  375 us
    all_gather x1, waiting for transfers between devices, body(): left_block = lax.all_gather(factor_left, 'pcol', axis=1, tiled=True).T  36.2 us
    dot_general x1, matrix products, body(): jnp.dot(left_rows, right_panel, precision=lax.Precision.HIGHEST, preferre...  36 us
    unnamed x10, local copies, waits for them, and re-layouts  33.5 us
    mul x1, local copies, waits for them, and re-layouts, body(): corrected * lax.rsqrt(jnp.sqrt(row_mean[:, None] * col_mean[None, :]))  33.3 us
    all_to_all x1, local copies, waits for them, and re-layouts, deal_columns(): lax.all_to_all(arranged, 'pcol', split_axis=1, concat_axis=0, tiled=True)  31.7 us
    all_to_all x1, local copies, waits for them, and re-layouts, body(): lax.all_to_all(order_rows(dealt), 'prow', split_axis=0, concat_axis=0, ti...  31.1 us
  transfers between devices with their start and end apart: 7, of which 5 were waited for; matrix products, arithmetic and copies ran while one was open for 4% of the time, Pallas kernels for 0%

profile of v1, /device:TPU:0, one launch (start us, length us, event | category | flops | bytes accessed | tf_op | source)
XLA Modules:
  0.0 1416.9 jit_solution(12684092029813159158)
XLA Ops:
  6.5 33.4 %copy.12 = f32[512,16384]{0,1:T(8,128)} copy(f32[512,16384]{1,0:T(8,128)} %param.3) | data formatting | bytes 67108864 | tf_op args[0]
  40.0 23.8 %copy.13 = f32[512,8,32,64]{0,3,2,1:T(8,128)} copy(f32[512,8,32,64]{0,3,1,2:T(8,128)} %bitcast.28) | data formatting | bytes 67108864 | tf_op jit(solution)/shard_map/transpose | solution.py:27
  63.7 7.1 all-to-all-start
  70.8 0.0 all-gather.2.cloned.1.call-start
  70.9 0.7 all-gather.2.cloned.1.call-update
  71.5 36.2 %all-gather.2.cloned.1.call-done = f32[64,4096]{1,0:T(8,128)} async-done(((f32[64,512]{1,0:T(8,128)}), f32[64,4096]{1,0:T(8,128)}) %all-gather.2.cloned.1.call-update) | async-done | bytes 1048592 | tf_op jit(solution)/shard_map/all_gather | solution.py:44
  107.8 2.6 reshape.27
  110.4 1.5 copy.23
  111.9 2.8 all_to_all.34
  114.6 688.6 %all-to-all-done = f32[512,8,2048]{0,2,1:T(8,128)} async-done(((f32[512,8,2048]{0,2,1:T(8,128)}), f32[512,8,2048]{0,2,1:T(8,128)}, u32[]{:S(2)}, u32[]{:S(2)}) %all-to-all-start) | async-done | bytes 33554464 | tf_op jit(solution)/shard_map/all_to_all | solution.py:30
  803.3 4.3 all-to-all-start.2
  807.6 31.7 %copy.14 = f32[8,512,2048]{2,1,0:T(8,128)} copy(f32[8,512,2048]{1,2,0:T(8,128)} %bitcast.3) | data formatting | bytes 67108864 | tf_op jit(solution)/shard_map/all_to_all | solution.py:30
  839.3 23.0 %copy.15 = f32[4,16,64,2048]{3,2,1,0:T(8,128)} copy(f32[4,16,64,2048]{3,2,0,1:T(8,128)} %bitcast.27) | data formatting | bytes 67108864 | tf_op jit(solution)/shard_map/transpose | solution.py:38
  862.3 0.0 all-to-all-done.2
  862.3 0.0 copy-start
  862.3 9.8 all-to-all-start.1
  872.2 0.0 copy-done
  872.2 2.1 collective-permute-start
  874.2 363.2 %collective-permute-done = f32[16,2048]{1,0:T(8,128)S(1)} collective-permute-done((f32[16,2048]{1,0:T(8,128)S(1)}, f32[16,2048]{1,0:T(8,128)S(1)}, u32[]{:S(2)}, u32[]{:S(2)}) %collective-permute-start) | collective-permute-done | bytes 131104 | tf_op jit(solution)/shard_map/ppermute | solution.py:15
  1237.5 0.0 collective-permute-start.1
  1237.5 5.9 collective-permute-done.1
  1243.3 0.0 collective-permute-start.2
  1243.4 5.9 collective-permute-done.2
  1249.4 0.1 copy.21
  1249.5 0.0 all-to-all-done.1
  1249.5 31.1 %copy.20 = f32[4096,2048]{0,1:T(8,128)} copy(f32[4096,2048]{1,0:T(8,128)} %bitcast.7) | data formatting | bytes 67108864 | tf_op jit(solution)/shard_map/all_to_all | solution.py:46
  1280.6 36.0 %multiply_reduce_fusion.1 = (f32[4096]{0:T(1024)S(1)}, f32[2048]{0:T(1024)S(1)}, f32[4096,2048]{0,1:T(8,128)}) fusion(f32[4096,2048]{0,1:T(8,128)} %copy.20, f32[4096,64]{0,1:T(8,128)S(1)} %bitcast.30, f32[128,2048]{1,0:T(8,128)S(1)} %constant_dynamic-update-slice_fusion, s32[]{:T(128)S(6)} %select_n.14), kind=kOutput, calls=%fused_computation.3 | convolution fusion | flops 6475999232 | bytes 68706304 | tf_op jit(solution)/shard_map/dot_general | solution.py:49
  1316.6 7.6 psum.15
  1324.2 25.9 %psum.14 = f32[4096]{0:T(1024)S(1)} all-reduce(f32[4096]{0:T(1024)S(1)} %get-tuple-element.5), channel_id=1, replica_groups=mesh['prow'=4,'pcol'=8] {'pcol'}, use_global_device_ids=true, to_apply=%region_1.2 | all-reduce | flops 4096 | bytes 32768 | tf_op jit(solution)/shard_map/psum | solution.py:53
  1350.1 26.6 %rsqrt_multiply_fusion = f32[4096,2048]{0,1:T(8,128)} fusion(f32[4096,2048]{0,1:T(8,128)} %get-tuple-element.7, f32[2048]{0:T(1024)S(1)} %multiply_add_fusion.1, f32[4096]{0:T(1024)S(1)} %multiply_add_fusion), kind=kLoop, calls=%fused_computation.1 | loop fusion | flops 16777216 | bytes 67133440 | tf_op jit(solution)/shard_map/mul | solution.py:57
  1376.7 33.3 %copy.19 = f32[4096,2048]{1,0:T(8,128)} copy(f32[4096,2048]{0,1:T(8,128)} %rsqrt_multiply_fusion) | data formatting | bytes 67108864 | tf_op jit(solution)/shard_map/mul | solution.py:57
  (10 shorter events, 0.1 us)
Async XLA Ops:
  63.7 739.6 %all-to-all-start = ((f32[512,8,2048]{0,2,1:T(8,128)}), f32[512,8,2048]{0,2,1:T(8,128)}, u32[]{:S(2)}, u32[]{:S(2)}) async-start(f32[512,8,2048]{0,2,1:T(8,128)} %bitcast.26), calls=%async_computation | async-start | bytes 67108864 | tf_op jit(solution)/shard_map/all_to_all | solution.py:30
  70.8 37.0 %all-gather.2.cloned.1.call-start = ((), (), s32[]{:S(2)}) async-start(), calls=%async_computation.3 | async-start | bytes 1179648 | tf_op jit(solution)/shard_map/all_gather | solution.py:44
  803.3 59.0 %all-to-all-start.2 = ((f32[4,1024,64]{1,2,0:T(8,128)}), f32[4,1024,64]{1,2,0:T(8,128)S(1)}, u32[]{:S(2)}, u32[]{:S(2)}) async-start(f32[4,1024,64]{1,2,0:T(8,128)} %all_to_all.34), calls=%async_computation.2 | async-start | bytes 2097152 | tf_op jit(solution)/shard_map/all_to_all | solution.py:47
  862.3 9.8 copy-start
  862.3 387.1 %all-to-all-start.1 = ((f32[4,1024,2048]{2,1,0:T(8,128)}), f32[4,1024,2048]{2,1,0:T(8,128)}, u32[]{:S(2)}, u32[]{:S(2)}) async-start(f32[4,1024,2048]{2,1,0:T(8,128)} %bitcast.25), calls=%async_computation.1 | async-start | bytes 67108864 | tf_op jit(solution)/shard_map/all_to_all | solution.py:46
  872.2 365.3 %collective-permute-start = (f32[16,2048]{1,0:T(8,128)S(1)}, f32[16,2048]{1,0:T(8,128)S(1)}, u32[]{:S(2)}, u32[]{:S(2)}) collective-permute-start(f32[16,2048]{1,0:T(8,128)S(1)} %copy-done), channel_id=1, source_target_pairs={{0,8},{8,16},{16,24},{24,0},{1,9},{9,17},{17,25},{25,1},{2,10},{10... | collective-permute-start | bytes 393224 | tf_op jit(solution)/shard_map/ppermute | solution.py:15
  1237.5 5.9 collective-permute-start.1
  1243.3 5.9 collective-permute-start.2
Sparse Core Ops, SparseCore 0:
  73.2 34.4 all-gather.1
